TPU v7x, 32 devices: a whole 2x2x4 slice. The times are simulated.
32 devices in a mesh: groups: 2 (over y), tmpl: 8 (over z, x), det: 2 (over core).
Axes of the slice: x: 2, y: 2, z: 4, core: 2. Of those that a mesh axis runs over, the one named last changes fastest.
Arguments:
- basis_series: bfloat16 [3, 128, 32768], P(None, None, ('groups', 'tmpl', 'det')), parts along dimension 2, may hold values from -6 to 6
- reconstruction: bfloat16 [3, 256, 2, 128], P(None, ('groups', 'tmpl')), parts along dimension 1, may hold values from -0.5 to 0.5
- offsets: int32 [6], P('groups'), parts along dimension 0, may hold values from 1024 to 16383
Outputs:
- window_peaks: float32 [128, 256], P(None, ('groups', 'tmpl', 'det')), parts along dimension 1
There are 2 independent parts, one for each index of `groups`. A program takes and returns all parts, laid end to end along the dimension named above; each array names one. Nothing has to cross between parts.
Inputs may be any that keep to these rules, and one draw needn't show every extreme that they name: `offsets`: slides are applied circularly over the segment's 16384 samples.
All inputs are finite; a program needn't handle non-finite values.
Results may differ from a plain program's by a relative error of at most 0.0003.
Values may be sent and summed in bfloat16 or wider, within the bound.
A program may use at most 64 MiB of HBM per device.

v0:
```python
import math

import jax
import jax.numpy as jnp
from jax import lax
from jax.sharding import PartitionSpec as P

DETS = 3
WIN = 128
SLIDE_BITS = 4


def from_behind(value, axis, steps):
    count = lax.axis_size(axis)
    pairs = [(source, (source + steps) % count) for source in range(count)]
    return lax.ppermute(value, axis, pairs)


def per_device(basis_series, reconstruction, offsets):
    block_len = basis_series.shape[2]
    blocks_moved = offsets // block_len
    remainder = offsets % block_len
    current_series = basis_series
    for bit_level in range(SLIDE_BITS):
        shifted = from_behind(current_series, ("tmpl", "det"), -(1 << bit_level))
        chosen = jnp.right_shift(blocks_moved, bit_level) % 2 == 1
        current_series = jnp.where(chosen[:, None, None], shifted, current_series)
    following = from_behind(current_series, ("tmpl", "det"), -1)
    joined = jnp.concatenate([current_series, following], axis=2)
    slid_series = jnp.stack(
        [
            lax.dynamic_slice_in_dim(joined[detector], remainder[detector], block_len, 1)
            for detector in range(DETS)
        ]
    )

    def peaks_of(bank_block):
        row_count = bank_block.shape[1]
        power_sum = jnp.zeros((row_count, block_len), jnp.float32)
        for detector in range(DETS):
            filtered = jnp.dot(
                bank_block[detector].reshape(row_count * 2, bank_block.shape[3]),
                slid_series[detector],
                preferred_element_type=jnp.float32,
            )
            filtered = filtered.reshape(row_count, 2, block_len)
            power_sum = power_sum + jnp.sum(filtered * filtered, axis=1)
        network = jnp.sqrt(power_sum)
        return jnp.max(network.reshape(row_count, block_len // WIN, WIN), axis=2)

    bank_piece = lax.all_gather(reconstruction, "tmpl", axis=1, tiled=True)
    row_count = bank_piece.shape[1]
    group_rows = math.gcd(row_count, 32)
    group_count = row_count // group_rows
    grouped = bank_piece.reshape(
        bank_piece.shape[0], group_count, group_rows, 2, bank_piece.shape[3]
    ).transpose(1, 0, 2, 3, 4)
    result = lax.map(peaks_of, grouped)
    return result.reshape(row_count, block_len // WIN)


def solution(mesh):
    in_specs = (
        P(None, None, ("groups", "tmpl", "det")),
        P(None, ("groups", "tmpl"), None, None),
        P("groups"),
    )
    out_specs = P(None, ("groups", "tmpl", "det"))
    return jax.shard_map(
        per_device, mesh=mesh, in_specs=in_specs, out_specs=out_specs, check_vma=False
    )
```

profile of v0, /device:TPU:0, one launch (start us, length us, event | category | flops | bytes accessed | tf_op | source)
XLA Modules:
  0.0 135.5 jit_solution(2438797000778645935)
XLA Ops:
  0.0 5.4 %collective-permute-start = (bf16[3,128,1024]{2,1,0:T(8,128)(2,1)}, bf16[3,128,1024]{2,1,0:T(8,128)(2,1)S(1)}, u32[]{:S(2)}, u32[]{:S(2)}) collective-permute-start(bf16[3,128,1024]{2,1,0:T(8,128)(2,1)} %param.5), channel_id=1, source_target_pairs={{0,15},{1,0},{2,1},{3,2},{4,3},{5,4},{6,5},{7,6},{8,7},{9,8},{10,9... | collective-permute-start | bytes 2359304 | tf_op jit(solution)/shard_map/ppermute | solution.py:16
  5.4 0.7 fusion.10
  6.1 9.1 %collective-permute-done = bf16[3,128,1024]{2,1,0:T(8,128)(2,1)S(1)} collective-permute-done((bf16[3,128,1024]{2,1,0:T(8,128)(2,1)}, bf16[3,128,1024]{2,1,0:T(8,128)(2,1)S(1)}, u32[]{:S(2)}, u32[]{:S(2)}) %collective-permute-start) | collective-permute-done | bytes 786464 | tf_op jit(solution)/shard_map/ppermute | solution.py:16
  15.3 1.3 broadcast_select_fusion
  16.6 0.6 collective-permute-start.1
  17.2 17.2 %collective-permute-done.1 = bf16[3,128,1024]{2,1,0:T(8,128)(2,1)S(1)} collective-permute-done((bf16[3,128,1024]{2,1,0:T(8,128)(2,1)S(1)}, bf16[3,128,1024]{2,1,0:T(8,128)(2,1)S(1)}, u32[]{:S(2)}, u32[]{:S(2)}) %collective-permute-start.1) | collective-permute-done | bytes 786464 | tf_op jit(solution)/shard_map/ppermute | solution.py:16
  34.4 0.1 broadcast_select_fusion.1
  34.5 0.9 collective-permute-start.2
  35.4 19.5 %collective-permute-done.2 = bf16[3,128,1024]{2,1,0:T(8,128)(2,1)S(1)} collective-permute-done((bf16[3,128,1024]{2,1,0:T(8,128)(2,1)S(1)}, bf16[3,128,1024]{2,1,0:T(8,128)(2,1)S(1)}, u32[]{:S(2)}, u32[]{:S(2)}) %collective-permute-start.2) | collective-permute-done | bytes 786464 | tf_op jit(solution)/shard_map/ppermute | solution.py:16
  54.9 0.1 broadcast_select_fusion.2
  55.0 1.1 collective-permute-start.3
  56.1 36.0 %collective-permute-done.3 = bf16[3,128,1024]{2,1,0:T(8,128)(2,1)S(1)} collective-permute-done((bf16[3,128,1024]{2,1,0:T(8,128)(2,1)S(1)}, bf16[3,128,1024]{2,1,0:T(8,128)(2,1)S(1)}, u32[]{:S(2)}, u32[]{:S(2)}) %collective-permute-start.3) | collective-permute-done | bytes 786464 | tf_op jit(solution)/shard_map/ppermute | solution.py:16
  92.2 0.0 copy-start.1
  92.2 0.0 copy-start
  92.2 0.1 broadcast_select_fusion.3
  92.3 1.2 collective-permute-start.4
  93.6 0.0 copy-done.1
  93.6 0.7 fusion.18
  98.0 0.0 copy-done
  99.9 30.6 %all_gather.3 = bf16[3,128,2,128]{3,1,2,0:T(8,128)(2,1)S(1)} all-gather(bf16[3,16,2,128]{3,1,2,0:T(8,128)(2,1)S(1)} %copy.8), channel_id=1, replica_groups=mesh['groups'=2,'tmpl'=8,'det'=2] {'tmpl'}, dimensions={1}, use_global_device_ids=true | all-gather | bytes 221184 | tf_op jit(solution)/shard_map/all_gather | solution.py:51
  130.5 0.1 pad_slice_fusion.3
  130.6 0.0 collective-permute-done.4
  130.6 0.1 pad_slice_fusion.1
  130.8 0.6 fusion.8
  131.3 0.3 fusion.7
  131.6 3.2 %while.10 = (s32[]{:T(128)}, f32[4,32,8]{2,1,0:T(8,128)S(1)}, bf16[4,3,32,2,128]{4,2,0,3,1:T(8,128)(2,1)S(1)}, bf16[128,1024]{1,0:T(8,128)(2,1)S(1)}, bf16[128,1...) while((s32[]{:T(128)}, f32[4,32,8]{2,1,0:T(8,128)S(1)}, ...), condition=%wide.region_5.6_spmd, body=%wide.region_0.5_spmd.sunk | while | flops 50724608 | bytes 2278497 | solution.py:58
  131.6 0.2 fusion.28
  131.8 0.2 fusion.29
  132.0 0.2 fusion.30
  132.3 0.1 reduce_max.10
  132.4 0.2 fusion.28
  132.6 0.2 fusion.29
  132.8 0.2 fusion.30
  133.1 0.1 reduce_max.10
  133.2 0.2 fusion.28
  133.4 0.2 fusion.29
  133.6 0.2 fusion.30
  133.9 0.1 reduce_max.10
  134.0 0.2 fusion.28
  134.2 0.2 fusion.29
  134.4 0.2 fusion.30
  134.7 0.1 reduce_max.10
  134.8 0.7 copy.11
  (20 shorter events, 0.4 us)
Async XLA Ops:
  0.0 15.3 %collective-permute-start = (bf16[3,128,1024]{2,1,0:T(8,128)(2,1)}, bf16[3,128,1024]{2,1,0:T(8,128)(2,1)S(1)}, u32[]{:S(2)}, u32[]{:S(2)}) collective-permute-start(bf16[3,128,1024]{2,1,0:T(8,128)(2,1)} %param.5), channel_id=1, source_target_pairs={{0,15},{1,0},{2,1},{3,2},{4,3},{5,4},{6,5},{7,6},{8,7},{9,8},{10,9... | collective-permute-start | bytes 2359304 | tf_op jit(solution)/shard_map/ppermute | solution.py:16
  16.6 17.8 %collective-permute-start.1 = (bf16[3,128,1024]{2,1,0:T(8,128)(2,1)S(1)}, bf16[3,128,1024]{2,1,0:T(8,128)(2,1)S(1)}, u32[]{:S(2)}, u32[]{:S(2)}) collective-permute-start(bf16[3,128,1024]{2,1,0:T(8,128)(2,1)S(1)} %broadcast_select_fusion), channel_id=1, source_target_pairs={{0,14},{1,15},{2,0},{3,1},{4,2},{5,3},{6,4},{7,5},{8,6},{9,7},{10,... | collective-permute-start | bytes 2359304 | tf_op jit(solution)/shard_map/ppermute | solution.py:16
  34.5 20.3 %collective-permute-start.2 = (bf16[3,128,1024]{2,1,0:T(8,128)(2,1)S(1)}, bf16[3,128,1024]{2,1,0:T(8,128)(2,1)S(1)}, u32[]{:S(2)}, u32[]{:S(2)}) collective-permute-start(bf16[3,128,1024]{2,1,0:T(8,128)(2,1)S(1)} %broadcast_select_fusion.1), channel_id=1, source_target_pairs={{0,12},{1,13},{2,14},{3,15},{4,0},{5,1},{6,2},{7,3},{8,4},{9,5},{1... | collective-permute-start | bytes 2359304 | tf_op jit(solution)/shard_map/ppermute | solution.py:16
  55.0 37.2 %collective-permute-start.3 = (bf16[3,128,1024]{2,1,0:T(8,128)(2,1)S(1)}, bf16[3,128,1024]{2,1,0:T(8,128)(2,1)S(1)}, u32[]{:S(2)}, u32[]{:S(2)}) collective-permute-start(bf16[3,128,1024]{2,1,0:T(8,128)(2,1)S(1)} %broadcast_select_fusion.2), channel_id=1, source_target_pairs={{0,8},{1,9},{2,10},{3,11},{4,12},{5,13},{6,14},{7,15},{8,0},{9,1},... | collective-permute-start | bytes 2359304 | tf_op jit(solution)/shard_map/ppermute | solution.py:16
  92.2 1.4 %copy-start.1 = (s32[3]{0:T(128)S(1)}, s32[3]{0:T(128)}, u32[]{:S(2)}) copy-start(s32[3]{0:T(128)} %param.7) | copy-start | bytes 40
  92.2 5.8 %copy-start = (bf16[3,16,2,128]{3,2,1,0:T(2,128)(2,1)S(1)}, bf16[3,16,2,128]{3,2,1,0:T(2,128)(2,1)}, u32[]{:S(2)}) copy-start(bf16[3,16,2,128]{3,2,1,0:T(2,128)(2,1)} %param.6) | copy-start | bytes 73732
  92.3 38.3 %collective-permute-start.4 = (bf16[3,128,1024]{2,1,0:T(8,128)(2,1)S(1)}, bf16[3,128,1024]{2,1,0:T(8,128)(2,1)S(1)}, u32[]{:S(2)}, u32[]{:S(2)}) collective-permute-start(bf16[3,128,1024]{2,1,0:T(8,128)(2,1)S(1)} %broadcast_select_fusion.3), channel_id=1, source_target_pairs={{0,15},{1,0},{2,1},{3,2},{4,3},{5,4},{6,5},{7,6},{8,7},{9,8},{10,9... | collective-permute-start | bytes 2359304 | tf_op jit(solution)/shard_map/ppermute | solution.py:16
where the time goes:
time: 136 us; the launch traced here: 135 us
  waiting for transfers between devices  81.9 us (60%)
  blocking collectives  30.6 us (22%)
  starting transfers between devices  9.29 us (7%)
  between operations  5.68 us (4%)
  other arithmetic  3.83 us (3%)
  matrix products  2.11 us (2%)
  local copies, waits for them, and re-layouts  1.74 us (1%)
    ppermute x5, waiting for transfers between devices, from_behind(): return lax.ppermute(value, axis, pairs)  81.9 us
    all_gather x1, blocking collectives, per_device(): bank_piece = lax.all_gather(reconstruction, 'tmpl', axis=1, tiled=True)  30.6 us
    ppermute x5, starting transfers between devices, from_behind(): return lax.ppermute(value, axis, pairs)  9.29 us
  transfers between devices with their start and end apart: 5, of which 4 were waited for; matrix products, arithmetic and copies ran while one was open for 1% of the time, Pallas kernels for 0%

commit v1 on v0

v1 whole, which is shorter than its diff:
```python
import functools
import math

import jax
import jax.numpy as jnp
from jax import lax
from jax.experimental import pallas as pl
from jax.experimental.pallas import tpu as pltpu
from jax.sharding import PartitionSpec as P

WIN = 128
MESH = pl.DeviceIdType.MESH
TINY = 1e-18
CODE = jnp.int16
SPAN = 30
STEPS = 1092
TOP = 15


def coded(power):
    log = jnp.log(jnp.maximum(power, 2.0 ** (TOP - 2 * SPAN))) * (STEPS / math.log(2.0))
    return jnp.round(log - (TOP - SPAN) * STEPS).astype(jnp.int32).astype(CODE)


def decoded(code):
    code = code.astype(jnp.int32).astype(jnp.float32)
    power = jnp.exp2(code * (1.0 / STEPS) + (TOP - SPAN))
    return jnp.where(code <= -SPAN * STEPS, 0.0, power)


def step_of(k, count):
    return count // 2 + (k // 2) * (2 * (k % 2) - 1)


def kernel(
    chips, cores,
    off_ref, basis_ref, bank_ref, out_ref,
    bank_all, stage, recv, dec, peaks, final,
    bank_s, bank_r, pow_s, pow_r, peak_s, peak_r,
):
    dets, basis, block = basis_ref.shape
    rows2 = bank_ref.shape[1] // cores
    rows = rows2 // 2
    half = block // 2
    wins = block // WIN
    count = chips * cores
    total = count * wins
    chip, core = lax.axis_index("tmpl"), lax.axis_index("det")
    me = chip * cores + core

    def dev(j, c):
        return {"tmpl": j, "det": c}

    top = jnp.max(jnp.abs(basis_ref[...]).astype(jnp.float32), axis=0)
    top = jnp.max(top, axis=0, keepdims=True)
    top = jnp.max(top, axis=1, keepdims=True)
    own = bank_ref[:, pl.ds(pl.multiple_of(core * rows2, rows2), rows2), :]
    bank_all[me, 0:dets] = own
    bank_all[me, dets] = jnp.broadcast_to(top, (rows2, WIN)).astype(jnp.bfloat16)
    own_max = jnp.max(jnp.max(jnp.max(jnp.abs(own).astype(jnp.float32), axis=0), axis=0, keepdims=True), axis=1, keepdims=True)

    barrier = pltpu.get_barrier_semaphore()

    @pl.loop(1, count)
    def _(k):
        t = lax.rem(me + k, count)
        pl.semaphore_signal(barrier, inc=1, device_id=dev(t // cores, lax.rem(t, cores)), device_id_type=MESH)

    pl.semaphore_wait(barrier, count - 1)

    def bank_copy(j, c, src):
        return pltpu.make_async_remote_copy(
            src_ref=bank_all.at[src], dst_ref=bank_all.at[src],
            send_sem=bank_s.at[j * cores + c], recv_sem=bank_r.at[src],
            device_id=dev(j, c), device_id_type=MESH)

    def pow_copy(j, c, src):
        return pltpu.make_async_remote_copy(
            src_ref=stage.at[j * cores + c], dst_ref=recv.at[src],
            send_sem=pow_s.at[j * cores + c], recv_sem=pow_r.at[src],
            device_id=dev(j, c), device_id_type=MESH)

    def peak_copy(j, c, src):
        return pltpu.make_async_remote_copy(
            src_ref=peaks.at[(j * cores + c) * wins // WIN], dst_ref=final.at[src],
            send_sem=peak_s.at[j * cores + c], recv_sem=peak_r.at[src],
            device_id=dev(j, c), device_id_type=MESH)

    def over_peers(fn, receive=False):
        for d in range(1, cores):
            fn(chip, lax.rem(core + d, cores))

        @pl.loop(1, chips)
        def _(k):
            s = step_of(k, chips)
            j = lax.rem(chip + chips - s, chips) if receive else lax.rem(chip + s, chips)
            for d in range(cores):
                fn(j, lax.rem(core + d, cores))

    over_peers(lambda j, c: bank_copy(j, c, me).start())

    size = cores * dets * rows2
    r = lax.broadcasted_iota(jnp.int32, (size, size), 0)
    i = lax.broadcasted_iota(jnp.int32, (size, size), 1)
    d_of = lax.div(r, cores * rows2)
    c_of = lax.rem(lax.div(r, rows2), cores)
    k_of = lax.rem(lax.div(r, rows), 2)
    m_of = lax.rem(r, rows)
    perm = (i == c_of * (dets * rows2) + d_of * rows2 + m_of * 2 + k_of).astype(jnp.float32).astype(jnp.bfloat16)

    def power_for(j):
        halves = [bank_all[j * cores + c, 0:dets].reshape(dets * rows2, basis) for c in range(cores)]
        invs = []
        for h in halves:
            b = jnp.max(jnp.abs(h).astype(jnp.float32), axis=0, keepdims=True)
            b = jnp.max(b, axis=1, keepdims=True)
            a = jnp.maximum(b * top, TINY)
            invs.append(1.0 / (a * a))
        w = jnp.dot(perm, jnp.concatenate(halves, axis=0), preferred_element_type=jnp.float32).astype(jnp.bfloat16)
        for d in range(dets):
            f = jnp.dot(w[d * cores * rows2:(d + 1) * cores * rows2], basis_ref[d], preferred_element_type=jnp.float32)
            f = f * f
            for c in range(cores):
                p = (f[c * rows2:c * rows2 + rows] + f[c * rows2 + rows:(c + 1) * rows2]) * invs[c]
                stage[j * cores + c, d] = coded(jnp.concatenate([p[:, :half], p[:, half:]], axis=0))

    for d in range(1, cores):
        bank_copy(chip, core, chip * cores + lax.rem(core + d, cores)).wait_recv()
    power_for(chip)
    for d in range(1, cores):
        pow_copy(chip, lax.rem(core + d, cores), me).start()

    @pl.loop(1, chips)
    def _(k):
        s = step_of(k, chips)
        j = lax.rem(chip + s, chips)
        for c in range(cores):
            bank_copy(chip, core, j * cores + c).wait_recv()
        power_for(j)
        for d in range(cores):
            pow_copy(j, lax.rem(core + d, cores), me).start()

    def decode(src, value):
        a = bank_all[src, dets].astype(jnp.float32)[0:rows]
        a = jnp.maximum(a * own_max, TINY)
        scale = a * a
        for d in range(dets):
            x = decoded(value(d))
            rest = lax.rem(off_ref[d], WIN)
            for v in range(wins):
                h, q = divmod(v, wins // 2)
                tile = x[h * rows:(h + 1) * rows, q * WIN:(q + 1) * WIN] * scale
                dec[d, src * wins + v] = pltpu.roll(tile, WIN - rest, 1)

    decode(me, lambda d: stage[me, d])

    def take(j, c):
        src = j * cores + c
        pow_copy(chip, core, src).wait_recv()
        decode(src, lambda d: recv[src, d])

    over_peers(take, receive=True)

    lane = lax.broadcasted_iota(jnp.int32, (rows, WIN), 1)
    shifts = [lax.div(off_ref[d], WIN) for d in range(dets)]
    keep = [lane < WIN - lax.rem(off_ref[d], WIN) for d in range(dets)]
    unroll = 16

    @pl.loop(0, total // WIN)
    def _(g):
        def body(u, acc):
            for v in range(unroll):
                at = u * unroll + v
                w = g * WIN + at
                power = None
                for d in range(dets):
                    first = lax.rem(w + shifts[d], total)
                    second = lax.rem(w + shifts[d] + 1, total)
                    x = jnp.where(keep[d], dec[d, first], dec[d, second])
                    power = x if power is None else power + x
                acc = jnp.where(lane == at, jnp.max(power, axis=1, keepdims=True), acc)
            return acc

        acc = lax.fori_loop(0, WIN // unroll, body, jnp.zeros((rows, WIN), jnp.float32))
        peaks[g] = jnp.sqrt(acc)

    over_peers(lambda j, c: peak_copy(j, c, me).start())

    def put(src, tile):
        tile = pltpu.roll(tile, lax.rem(WIN - lax.rem(me * wins, WIN), WIN), 1)
        out_ref[pl.ds(pl.multiple_of(src * rows, rows), rows), :] = tile[:, :wins]

    put(me, peaks[me * wins // WIN])

    def collect(j, c):
        src = j * cores + c
        peak_copy(chip, core, src).wait_recv()
        put(src, final[src])

    over_peers(collect, receive=True)

    def drain(j, c):
        bank_copy(j, c, me).wait_send()
        pow_copy(j, c, me).wait_send()
        peak_copy(j, c, me).wait_send()

    over_peers(drain)


def per_device(chips, cores, basis_series, reconstruction, offsets):
    dets, basis, block = basis_series.shape
    templates = reconstruction.shape[1]
    bank = reconstruction.reshape(dets, templates * 2, basis)
    count = chips * cores
    rows = templates // cores
    wins = block // WIN
    total = count * wins
    vmem = pl.BlockSpec(memory_space=pltpu.VMEM)
    return pl.pallas_call(
        functools.partial(kernel, chips, cores),
        out_shape=jax.ShapeDtypeStruct((count * rows, wins), jnp.float32),
        in_specs=[pl.BlockSpec(memory_space=pltpu.SMEM), vmem, vmem],
        out_specs=vmem,
        scratch_shapes=[
            pltpu.VMEM((count, dets + 1, rows * 2, basis), jnp.bfloat16),
            pltpu.VMEM((count, dets, rows * 2, block // 2), CODE),
            pltpu.VMEM((count, dets, rows * 2, block // 2), CODE),
            pltpu.VMEM((dets, total, rows, WIN), jnp.float32),
            pltpu.VMEM((max(total // WIN, 1), rows, WIN), jnp.float32),
            pltpu.VMEM((count, rows, WIN), jnp.float32),
        ] + [pltpu.SemaphoreType.DMA((count,)) for _ in range(6)],
        compiler_params=pltpu.CompilerParams(
            collective_id=0, has_side_effects=True, vmem_limit_bytes=63_000_000),
    )(offsets, basis_series, bank)


def solution(mesh):
    chips, cores = mesh.shape["tmpl"], mesh.shape["det"]
    in_specs = (
        P(None, None, ("groups", "tmpl", "det")),
        P(None, ("groups", "tmpl"), None, None),
        P("groups"),
    )
    out_specs = P(None, ("groups", "tmpl", "det"))
    return jax.shard_map(
        functools.partial(per_device, chips, cores),
        mesh=mesh, in_specs=in_specs, out_specs=out_specs, check_vma=False,
    )
```

time: 136 us -> 41.9 us (0.31)
  waiting for transfers between devices: 81.9 us -> 0 us
  Pallas kernels: 0 us -> 40.2 us
  blocking collectives: 30.6 us -> 0 us
  starting transfers between devices: 9.29 us -> 0 us
  between operations: 5.68 us -> 0.01 us
  other arithmetic: 3.83 us -> 0 us
  matrix products: 2.11 us -> 0 us
    ppermute x5 -> x0, waiting for transfers between devices: 81.9 us -> none  [from_behind(): return lax.ppermute(value, axis, pairs)]
    pallas_call x0 -> x1, Pallas kernels: none -> 40.2 us  [per_device(): pl.pallas_call(functools.partial(kernel, chips, cores), out_shape=jax.Sha...]
    all_gather x1 -> x0, blocking collectives: 30.6 us -> none  [per_device(): bank_piece = lax.all_gather(reconstruction, 'tmpl', axis=1, tiled=True)]
    ppermute x5 -> x0, starting transfers between devices: 9.29 us -> none  [from_behind(): return lax.ppermute(value, axis, pairs)]
    dot_general x12 -> x0, matrix products: 2.11 us -> none  [peaks_of(): jnp.dot(bank_block[detector].reshape(row_count * 2, bank_block.shape[3]),...]
    select_n x5 -> x0, other arithmetic: 1.72 us -> none  [the longest x4 1.71 us: per_device(): current_series = jnp.where(chosen[:, None, None], shifted, current_series)]
    pallas_call x0 -> x1, local copies, waits for them, and re-layouts: none -> 1.5 us  [per_device(): pl.pallas_call(functools.partial(kernel, chips, cores), out_shape=jax.Sha...]
  transfers between devices with their start and end apart: 5 -> 0, of which waited for: 4 -> 0; matrix products, arithmetic and copies ran while one was open for 1% -> 0% of each run, Pallas kernels for 0% -> 0%
where the time goes in v1:
time: 41.9 us; the launch traced here: 41.7 us
  Pallas kernels  40.2 us (96%)
  local copies, waits for them, and re-layouts  1.5 us (4%)
    pallas_call x1, Pallas kernels, per_device(): pl.pallas_call(functools.partial(kernel, chips, cores), out_shape=jax.Sha...  40.2 us
    pallas_call x1, local copies, waits for them, and re-layouts, per_device(): pl.pallas_call(functools.partial(kernel, chips, cores), out_shape=jax.Sha...  1.5 us

profile of v1, /device:TPU:0, one launch (start us, length us, event | category | flops | bytes accessed | tf_op | source)
XLA Modules:
  0.0 41.7 jit_solution(15865965313946079063)
XLA Ops:
  0.0 40.2 %shard_map.37 = f32[128,8]{1,0:T(8,128)} custom-call(s32[3]{0:T(128)} %off_ref.1, bf16[3,128,1024]{2,1,0:T(8,128)(2,1)} %basis_ref.1, bf16[3,32,128]{2,1,0:T(8,128)(2,1)} %bitcast.1), custom_call_target="tpu_custom_call" | custom-call | tf_op jit(solution)/shard_map/pallas_call | solution.py:219
  40.2 1.5 %copy.4 = f32[128,8]{0,1:T(8,128)} copy(f32[128,8]{1,0:T(8,128)} %shard_map.37) | data formatting | bytes 8192 | tf_op jit(solution)/shard_map/pallas_call | solution.py:219

commit v2 on v1

v2 whole, which is shorter than its diff:
```python
import functools
import math

import jax
import jax.numpy as jnp
from jax import lax
from jax.experimental import pallas as pl
from jax.experimental.pallas import tpu as pltpu
from jax.sharding import PartitionSpec as P

WIN = 128
SLIDE_BLOCKS = 16
MESH = pl.DeviceIdType.MESH
TINY = 1e-18
CODE = jnp.int16
SPAN = 30
STEPS = 1092
TOP = 15


def coded(power):
    log = jnp.log(jnp.maximum(power, 2.0 ** (TOP - 2 * SPAN))) * (STEPS / math.log(2.0))
    return jnp.round(log - (TOP - SPAN) * STEPS).astype(jnp.int32).astype(CODE)


def decoded(code):
    code = code.astype(jnp.int32).astype(jnp.float32)
    power = jnp.exp2(code * (1.0 / STEPS) + (TOP - SPAN))
    return jnp.where(code <= -SPAN * STEPS, 0.0, power)


def step_of(k, count):
    return count // 2 + (k // 2) * (2 * (k % 2) - 1)


def kernel(
    chips, cores,
    off_ref, basis_hbm, bank_hbm, out_ref,
    basis_ref, bank_ref, bank_all, top_all, stage, recv, dec, peaks, final,
    load, bank_s, bank_r, pass_s, top_s, top_r, pow_s, pow_r, peak_s, peak_r,
):
    dets, basis, block = basis_ref.shape
    rows2 = bank_ref.shape[1] // cores
    rows = rows2 // 2
    half = block // 2
    wins = block // WIN
    count = chips * cores
    total = count * wins
    per_row = WIN // rows
    chip, core = lax.axis_index("tmpl"), lax.axis_index("det")
    me = chip * cores + core

    load_bank = pltpu.make_async_copy(bank_hbm, bank_ref, load.at[0])
    load_basis = pltpu.make_async_copy(basis_hbm, basis_ref, load.at[1])
    load_bank.start()
    load_basis.start()

    def dev(j, c):
        return {"tmpl": j, "det": c}

    def over_chips(fn, receive=False):
        @pl.loop(1, chips)
        def _(k):
            s = step_of(k, chips)
            fn(lax.rem(chip + chips - s, chips) if receive else lax.rem(chip + s, chips))

    def over_peers(fn, receive=False):
        for d in range(1, cores):
            fn(chip, lax.rem(core + d, cores))

        def each(j):
            for d in range(cores):
                fn(j, lax.rem(core + d, cores))

        over_chips(each, receive)

    barrier = pltpu.get_barrier_semaphore()
    over_peers(lambda j, c: pl.semaphore_signal(barrier, inc=1, device_id=dev(j, c), device_id_type=MESH))

    mine = pl.ds(pl.multiple_of(core * rows2, rows2), rows2)

    def bank_copy(j, src):
        return pltpu.make_async_remote_copy(
            src_ref=bank_ref.at[:, mine], dst_ref=bank_all.at[src],
            send_sem=bank_s.at[j], recv_sem=bank_r.at[src],
            device_id=dev(j, core), device_id_type=MESH)

    def pass_copy(src, c):
        return pltpu.make_async_remote_copy(
            src_ref=bank_all.at[src], dst_ref=bank_all.at[src],
            send_sem=pass_s.at[lax.div(src, cores) * cores + c], recv_sem=bank_r.at[src],
            device_id=dev(chip, c), device_id_type=MESH)

    def top_copy(j, c, src):
        return pltpu.make_async_remote_copy(
            src_ref=top_all.at[src], dst_ref=top_all.at[src],
            send_sem=top_s.at[j * cores + c], recv_sem=top_r.at[src],
            device_id=dev(j, c), device_id_type=MESH)

    def pow_copy(j, c, src):
        return pltpu.make_async_remote_copy(
            src_ref=stage.at[j * cores + c], dst_ref=recv.at[src],
            send_sem=pow_s.at[j * cores + c], recv_sem=pow_r.at[src],
            device_id=dev(j, c), device_id_type=MESH)

    def peak_copy(j, c, src):
        return pltpu.make_async_remote_copy(
            src_ref=peaks.at[(j * cores + c) * wins // per_row], dst_ref=final.at[src],
            send_sem=peak_s.at[j * cores + c], recv_sem=peak_r.at[src],
            device_id=dev(j, c), device_id_type=MESH)

    size = cores * dets * rows2
    r = lax.broadcasted_iota(jnp.int32, (size, size), 0)
    i = lax.broadcasted_iota(jnp.int32, (size, size), 1)
    d_of = lax.div(r, cores * rows2)
    c_of = lax.rem(lax.div(r, rows2), cores)
    k_of = lax.rem(lax.div(r, rows), 2)
    m_of = lax.rem(r, rows)
    perm = (i == c_of * (dets * rows2) + d_of * rows2 + m_of * 2 + k_of).astype(jnp.float32).astype(jnp.bfloat16)

    def largest(x):
        x = jnp.max(jnp.abs(x).astype(jnp.float32), axis=0)
        return jnp.max(jnp.max(x, axis=0, keepdims=True), axis=1, keepdims=True)

    load_bank.wait()
    load_basis.wait()
    top = largest(basis_ref[...])
    top_all[me] = jnp.broadcast_to(top, (1, WIN))
    own_max = largest(bank_ref[:, mine])

    def power_for(j, halves):
        invs = []
        for h in halves:
            a = jnp.maximum(largest(h) * top, TINY)
            invs.append(1.0 / (a * a))
        w = jnp.concatenate([h.reshape(dets * rows2, basis) for h in halves], axis=0)
        w = jnp.dot(perm, w, preferred_element_type=jnp.float32).astype(jnp.bfloat16)
        for d in range(dets):
            f = jnp.dot(w[d * cores * rows2:(d + 1) * cores * rows2], basis_ref[d], preferred_element_type=jnp.float32)
            f = f * f
            for c in range(cores):
                p = (f[c * rows2:c * rows2 + rows] + f[c * rows2 + rows:(c + 1) * rows2]) * invs[c]
                stage[j * cores + c, d] = coded(jnp.concatenate([p[:, :half], p[:, half:]], axis=0))

    power_for(chip, [bank_ref[:, c * rows2:(c + 1) * rows2] for c in range(cores)])

    pl.semaphore_wait(barrier, count - 1)
    over_chips(lambda j: bank_copy(j, me).start())
    over_peers(lambda j, c: top_copy(j, c, me).start())
    for d in range(1, cores):
        pow_copy(chip, lax.rem(core + d, cores), me).start()

    def pass_on(k):
        src = lax.rem(chip + step_of(k, chips), chips) * cores + core
        bank_copy(chip, src).wait_recv()
        for d in range(1, cores):
            pass_copy(src, lax.rem(core + d, cores)).start()

    pass_on(1)

    @pl.loop(1, chips)
    def _(k):
        @pl.when(k < chips - 1)
        def _():
            pass_on(k + 1)

        j = lax.rem(chip + step_of(k, chips), chips)
        for d in range(1, cores):
            bank_copy(chip, j * cores + lax.rem(core + d, cores)).wait_recv()
        power_for(j, [bank_all[j * cores + c] for c in range(cores)])
        for d in range(cores):
            pow_copy(j, lax.rem(core + d, cores), me).start()

    rest = [lax.rem(off_ref[d], WIN) for d in range(dets)]
    shifts = [lax.div(off_ref[d], WIN) for d in range(dets)]

    def decode(src, value):
        a = jnp.maximum(top_all[src] * own_max, TINY)
        scale = a * a
        for d in range(dets):
            x = decoded(value(d))
            tiles = []
            for v in range(wins):
                h, q = divmod(v, wins // 2)
                tile = x[h * rows:(h + 1) * rows, q * WIN:(q + 1) * WIN] * scale
                tile = pltpu.roll(tile, WIN - rest[d], 1)
                dec[d, src * wins + v] = tile
                tiles.append(tile)

            @pl.when(src < SLIDE_BLOCKS)
            def _():
                for v in range(wins):
                    dec[d, (count + src) * wins + v] = tiles[v]

    decode(me, lambda d: stage[me, d])

    def take(j, c):
        src = j * cores + c
        top_copy(chip, core, src).wait_recv()
        pow_copy(chip, core, src).wait_recv()
        decode(src, lambda d: recv[src, d])

    over_peers(take, receive=True)

    lane = lax.broadcasted_iota(jnp.int32, (per_row, rows, WIN), 2)

    @pl.loop(0, total // per_row)
    def _(g):
        power = None
        for d in range(dets):
            tiles = dec[d, pl.ds(g * per_row + shifts[d], per_row + 1)]
            x = jnp.where(lane < WIN - rest[d], tiles[:per_row], tiles[1:])
            power = x if power is None else power + x
        turned = power.reshape(per_row * rows, WIN).T
        peaks[g] = jnp.sqrt(jnp.max(turned, axis=0, keepdims=True))

    over_peers(lambda j, c: peak_copy(j, c, me).start())
    final[me] = peaks[me * wins // per_row]
    over_peers(lambda j, c: peak_copy(chip, core, j * cores + c).wait_recv(), receive=True)

    base = lax.rem(me * wins, per_row) * rows
    e_of = lax.broadcasted_iota(jnp.int32, (per_row, WIN), 0)
    l_of = lax.broadcasted_iota(jnp.int32, (per_row, WIN), 1)
    for g in range(count // per_row):
        x = final[g * per_row:(g + 1) * per_row].reshape(per_row, WIN)
        x = pltpu.roll(x, lax.rem(WIN - base, WIN), 1)
        x = jnp.concatenate([
            pltpu.roll(x[h:h + 8], h * rows, 1, stride=rows, stride_axis=0) for h in range(0, per_row, 8)], axis=0)
        for i in range(wins):
            y = pltpu.roll(x, (WIN - i * rows) % WIN, 1)
            y = jnp.where(lax.div(l_of, rows) == e_of, y, 0.0)
            out_ref[i:i + 1, g * WIN:(g + 1) * WIN] = jnp.sum(y, axis=0, keepdims=True)

    over_chips(lambda j: bank_copy(j, me).wait_send())

    def passed(j):
        for d in range(1, cores):
            pass_copy(j * cores + core, lax.rem(core + d, cores)).wait_send()

    over_chips(passed)

    def drain(j, c):
        top_copy(j, c, me).wait_send()
        pow_copy(j, c, me).wait_send()
        peak_copy(j, c, me).wait_send()

    over_peers(drain)


def per_device(chips, cores, basis_series, reconstruction, offsets):
    dets, basis, block = basis_series.shape
    templates = reconstruction.shape[1]
    bank = reconstruction.reshape(dets, templates * 2, basis)
    count = chips * cores
    rows = templates // cores
    wins = block // WIN
    total = count * wins
    per_row = WIN // rows
    hbm = pl.BlockSpec(memory_space=pl.ANY)
    out = pl.pallas_call(
        functools.partial(kernel, chips, cores),
        out_shape=jax.ShapeDtypeStruct((wins, count * rows), jnp.float32),
        in_specs=[pl.BlockSpec(memory_space=pltpu.SMEM), hbm, hbm],
        out_specs=pl.BlockSpec(memory_space=pltpu.VMEM),
        scratch_shapes=[
            pltpu.VMEM(basis_series.shape, basis_series.dtype),
            pltpu.VMEM(bank.shape, bank.dtype),
            pltpu.VMEM((count, dets, rows * 2, basis), jnp.bfloat16),
            pltpu.VMEM((count, 1, WIN), jnp.float32),
            pltpu.VMEM((count, dets, rows * 2, block // 2), CODE),
            pltpu.VMEM((count, dets, rows * 2, block // 2), CODE),
            pltpu.VMEM((dets, total + SLIDE_BLOCKS * wins, rows, WIN), jnp.float32),
            pltpu.VMEM((total // per_row, 1, WIN), jnp.float32),
            pltpu.VMEM((count, 1, WIN), jnp.float32),
            pltpu.SemaphoreType.DMA((2,)),
            pltpu.SemaphoreType.DMA((chips,)),
        ] + [pltpu.SemaphoreType.DMA((count,)) for _ in range(8)],
        compiler_params=pltpu.CompilerParams(
            collective_id=0, has_side_effects=True, vmem_limit_bytes=63_000_000),
    )(offsets, basis_series, bank)
    return out.T


def solution(mesh):
    chips, cores = mesh.shape["tmpl"], mesh.shape["det"]
    in_specs = (
        P(None, None, ("groups", "tmpl", "det")),
        P(None, ("groups", "tmpl"), None, None),
        P("groups"),
    )
    out_specs = P(None, ("groups", "tmpl", "det"))
    return jax.shard_map(
        functools.partial(per_device, chips, cores),
        mesh=mesh, in_specs=in_specs, out_specs=out_specs, check_vma=False,
    )
```

time: 41.9 us -> 39.2 us (0.936)
  Pallas kernels: 40.2 us -> 37.7 us
    pallas_call x1, Pallas kernels: 40.2 us -> 37.7 us  [per_device(): pl.pallas_call(functools.partial(kernel, chips, cores), out_shape=jax.Sha...]
    pallas_call x1 -> x0, local copies, waits for them, and re-layouts: 1.5 us -> none  [per_device(): pl.pallas_call(functools.partial(kernel, chips, cores), out_shape=jax.Sha...]
    unnamed x0 -> x1, local copies, waits for them, and re-layouts: none -> 1.28 us
where the time goes in v2:
time: 39.2 us; the launch traced here: 39 us
  Pallas kernels  37.7 us (96%)
  local copies, waits for them, and re-layouts  1.28 us (3%)
    pallas_call x1, Pallas kernels, per_device(): pl.pallas_call(functools.partial(kernel, chips, cores), out_shape=jax.Sha...  37.7 us
    unnamed x1, local copies, waits for them, and re-layouts  1.28 us

profile of v2, /device:TPU:0, one launch (start us, length us, event | category | flops | bytes accessed | tf_op | source)
XLA Modules:
  0.0 39.0 jit_solution(6274987478684067419)
XLA Ops:
  0.0 37.7 %shard_map.37 = f32[8,128]{1,0:T(8,128)} custom-call(s32[3]{0:T(128)} %off_ref.1, bf16[3,128,1024]{2,1,0:T(8,128)(2,1)} %basis_hbm.1, bf16[3,32,128]{2,1,0:T(8,128)(2,1)} %bitcast.2), custom_call_target="tpu_custom_call" | custom-call | tf_op jit(solution)/shard_map/pallas_call | solution.py:260
  37.7 1.3 %copy.5 = f32[128,8]{0,1:T(8,128)} copy(f32[128,8]{0,1:T(8,128)} %bitcast.3) | data formatting | bytes 8192

commit v3 on v2

--- a/solution.py
+++ b/solution.py
@@ -29,8 +29,12 @@
     return jnp.where(code <= -SPAN * STEPS, 0.0, power)
 
 
-def step_of(k, count):
-    return count // 2 + (k // 2) * (2 * (k % 2) - 1)
+def partner(chip, chips, k, sign):
+    half = chips // 2
+    near = k // half
+    turn = k - near * half + near
+    side = lax.rem(lax.div(chip, half) + 1 - near, 2)
+    return side * half + lax.rem(lax.rem(chip, half) + half + sign * turn, half)
 
 
 def kernel(
@@ -58,21 +62,21 @@
     def dev(j, c):
         return {"tmpl": j, "det": c}
 
-    def over_chips(fn, receive=False):
-        @pl.loop(1, chips)
+    def over_chips(fn, sign=1, short=True):
+        if short and chips <= 8:
+            for k in range(chips - 1):
+                fn(partner(chip, chips, k, sign))
+            return
+
+        @pl.loop(0, chips - 1)
         def _(k):
-            s = step_of(k, chips)
-            fn(lax.rem(chip + chips - s, chips) if receive else lax.rem(chip + s, chips))
-
-    def over_peers(fn, receive=False):
+            fn(partner(chip, chips, k, sign))
+
+    def over_peers(fn, sign=1):
+        for d in range(cores):
+            over_chips(lambda j: fn(j, lax.rem(core + d, cores)), sign)
         for d in range(1, cores):
             fn(chip, lax.rem(core + d, cores))
-
-        def each(j):
-            for d in range(cores):
-                fn(j, lax.rem(core + d, cores))
-
-        over_chips(each, receive)
 
     barrier = pltpu.get_barrier_semaphore()
     over_peers(lambda j, c: pl.semaphore_signal(barrier, inc=1, device_id=dev(j, c), device_id_type=MESH))
@@ -109,14 +113,12 @@
             send_sem=peak_s.at[j * cores + c], recv_sem=peak_r.at[src],
             device_id=dev(j, c), device_id_type=MESH)
 
-    size = cores * dets * rows2
-    r = lax.broadcasted_iota(jnp.int32, (size, size), 0)
-    i = lax.broadcasted_iota(jnp.int32, (size, size), 1)
-    d_of = lax.div(r, cores * rows2)
-    c_of = lax.rem(lax.div(r, rows2), cores)
+    r = lax.broadcasted_iota(jnp.int32, (dets * rows2, dets * rows2), 0)
+    i = lax.broadcasted_iota(jnp.int32, (dets * rows2, dets * rows2), 1)
+    d_of = lax.div(r, rows2)
     k_of = lax.rem(lax.div(r, rows), 2)
     m_of = lax.rem(r, rows)
-    perm = (i == c_of * (dets * rows2) + d_of * rows2 + m_of * 2 + k_of).astype(jnp.float32).astype(jnp.bfloat16)
+    perm = (i == d_of * rows2 + m_of * 2 + k_of).astype(jnp.float32).astype(jnp.bfloat16)
 
     def largest(x):
         x = jnp.max(jnp.abs(x).astype(jnp.float32), axis=0)
@@ -128,21 +130,18 @@
     top_all[me] = jnp.broadcast_to(top, (1, WIN))
     own_max = largest(bank_ref[:, mine])
 
-    def power_for(j, halves):
-        invs = []
-        for h in halves:
-            a = jnp.maximum(largest(h) * top, TINY)
-            invs.append(1.0 / (a * a))
-        w = jnp.concatenate([h.reshape(dets * rows2, basis) for h in halves], axis=0)
-        w = jnp.dot(perm, w, preferred_element_type=jnp.float32).astype(jnp.bfloat16)
+    def power_for(to, bank):
+        a = jnp.maximum(largest(bank) * top, TINY)
+        inv = 1.0 / (a * a)
+        w = jnp.dot(perm, bank.reshape(dets * rows2, basis), preferred_element_type=jnp.float32).astype(jnp.bfloat16)
         for d in range(dets):
-            f = jnp.dot(w[d * cores * rows2:(d + 1) * cores * rows2], basis_ref[d], preferred_element_type=jnp.float32)
+            f = jnp.dot(w[d * rows2:(d + 1) * rows2], basis_ref[d], preferred_element_type=jnp.float32)
             f = f * f
-            for c in range(cores):
-                p = (f[c * rows2:c * rows2 + rows] + f[c * rows2 + rows:(c + 1) * rows2]) * invs[c]
-                stage[j * cores + c, d] = coded(jnp.concatenate([p[:, :half], p[:, half:]], axis=0))
-
-    power_for(chip, [bank_ref[:, c * rows2:(c + 1) * rows2] for c in range(cores)])
+            p = (f[:rows] + f[rows:]) * inv
+            stage[to, d] = coded(jnp.concatenate([p[:, :half], p[:, half:]], axis=0))
+
+    for c in range(cores):
+        power_for(chip * cores + c, bank_ref[:, c * rows2:(c + 1) * rows2])
 
     pl.semaphore_wait(barrier, count - 1)
     over_chips(lambda j: bank_copy(j, me).start())
@@ -150,26 +149,26 @@
     for d in range(1, cores):
         pow_copy(chip, lax.rem(core + d, cores), me).start()
 
-    def pass_on(k):
-        src = lax.rem(chip + step_of(k, chips), chips) * cores + core
+    def direct(j):
+        src = j * cores + core
         bank_copy(chip, src).wait_recv()
         for d in range(1, cores):
             pass_copy(src, lax.rem(core + d, cores)).start()
-
-    pass_on(1)
-
-    @pl.loop(1, chips)
-    def _(k):
-        @pl.when(k < chips - 1)
-        def _():
-            pass_on(k + 1)
-
-        j = lax.rem(chip + step_of(k, chips), chips)
-        for d in range(1, cores):
-            bank_copy(chip, j * cores + lax.rem(core + d, cores)).wait_recv()
-        power_for(j, [bank_all[j * cores + c] for c in range(cores)])
-        for d in range(cores):
-            pow_copy(j, lax.rem(core + d, cores), me).start()
+        power_for(src, bank_all[src])
+        pow_copy(j, core, me).start()
+
+    over_chips(direct, -1, short=False)
+
+    for d in range(1, cores):
+        other = lax.rem(core + d, cores)
+
+        def passed_on(j):
+            src = j * cores + other
+            bank_copy(chip, src).wait_recv()
+            power_for(src, bank_all[src])
+            pow_copy(j, other, me).start()
+
+        over_chips(passed_on, -1, short=False)
 
     rest = [lax.rem(off_ref[d], WIN) for d in range(dets)]
     shifts = [lax.div(off_ref[d], WIN) for d in range(dets)]
@@ -200,11 +199,14 @@
         pow_copy(chip, core, src).wait_recv()
         decode(src, lambda d: recv[src, d])
 
-    over_peers(take, receive=True)
+    for d in range(1, cores):
+        take(chip, lax.rem(core + d, cores))
+    for d in range(cores):
+        over_chips(lambda j: take(j, lax.rem(core + d, cores)), short=False)
 
     lane = lax.broadcasted_iota(jnp.int32, (per_row, rows, WIN), 2)
 
-    @pl.loop(0, total // per_row)
+    @pl.loop(0, total // per_row, unroll=4)
     def _(g):
         power = None
         for d in range(dets):
@@ -216,7 +218,7 @@
 
     over_peers(lambda j, c: peak_copy(j, c, me).start())
     final[me] = peaks[me * wins // per_row]
-    over_peers(lambda j, c: peak_copy(chip, core, j * cores + c).wait_recv(), receive=True)
+    over_peers(lambda j, c: peak_copy(chip, core, j * cores + c).wait_recv(), -1)
 
     base = lax.rem(me * wins, per_row) * rows
     e_of = lax.broadcasted_iota(jnp.int32, (per_row, WIN), 0)

time: 39.2 us -> 36.6 us (0.934)
  Pallas kernels: 37.7 us -> 35.1 us
    pallas_call x1, Pallas kernels: 37.7 us -> 35.1 us  [per_device(): pl.pallas_call(functools.partial(kernel, chips, cores), out_shape=jax.Sha...]
where the time goes in v3:
time: 36.6 us; the launch traced here: 36.4 us
  Pallas kernels  35.1 us (96%)
  local copies, waits for them, and re-layouts  1.28 us (3%)
    pallas_call x1, Pallas kernels, per_device(): pl.pallas_call(functools.partial(kernel, chips, cores), out_shape=jax.Sha...  35.1 us
    unnamed x1, local copies, waits for them, and re-layouts  1.28 us

profile of v3, /device:TPU:0, one launch (start us, length us, event | category | flops | bytes accessed | tf_op | source)
XLA Modules:
  0.0 36.4 jit_solution(14856355154409210157)
XLA Ops:
  0.0 35.1 %shard_map.37 = f32[8,128]{1,0:T(8,128)} custom-call(s32[3]{0:T(128)} %off_ref.1, bf16[3,128,1024]{2,1,0:T(8,128)(2,1)} %basis_hbm.1, bf16[3,32,128]{2,1,0:T(8,128)(2,1)} %bitcast.2), custom_call_target="tpu_custom_call" | custom-call | tf_op jit(solution)/shard_map/pallas_call | solution.py:262
  35.1 1.3 %copy.5 = f32[128,8]{0,1:T(8,128)} copy(f32[128,8]{0,1:T(8,128)} %bitcast.3) | data formatting | bytes 8192

commit v4 on v3

--- a/solution.py
+++ b/solution.py
@@ -39,8 +39,8 @@
 
 def kernel(
     chips, cores,
-    off_ref, basis_hbm, bank_hbm, out_ref,
-    basis_ref, bank_ref, bank_all, top_all, stage, recv, dec, peaks, final,
+    off_hbm, basis_hbm, bank_hbm, out_ref,
+    off_ref, basis_ref, bank_ref, bank_all, top_all, stage, recv, dec, peaks, final,
     load, bank_s, bank_r, pass_s, top_s, top_r, pow_s, pow_r, peak_s, peak_r,
 ):
     dets, basis, block = basis_ref.shape
@@ -56,8 +56,10 @@
 
     load_bank = pltpu.make_async_copy(bank_hbm, bank_ref, load.at[0])
     load_basis = pltpu.make_async_copy(basis_hbm, basis_ref, load.at[1])
+    load_off = pltpu.make_async_copy(off_hbm, off_ref, load.at[2])
     load_bank.start()
     load_basis.start()
+    load_off.start()
 
     def dev(j, c):
         return {"tmpl": j, "det": c}
@@ -126,6 +128,7 @@
 
     load_bank.wait()
     load_basis.wait()
+    load_off.wait()
     top = largest(basis_ref[...])
     top_all[me] = jnp.broadcast_to(top, (1, WIN))
     own_max = largest(bank_ref[:, mine])
@@ -258,13 +261,14 @@
     wins = block // WIN
     total = count * wins
     per_row = WIN // rows
-    hbm = pl.BlockSpec(memory_space=pl.ANY)
+    hbm = pl.BlockSpec(memory_space=pltpu.HBM)
     out = pl.pallas_call(
         functools.partial(kernel, chips, cores),
         out_shape=jax.ShapeDtypeStruct((wins, count * rows), jnp.float32),
-        in_specs=[pl.BlockSpec(memory_space=pltpu.SMEM), hbm, hbm],
+        in_specs=[hbm, hbm, hbm],
         out_specs=pl.BlockSpec(memory_space=pltpu.VMEM),
         scratch_shapes=[
+            pltpu.SMEM(offsets.shape, offsets.dtype),
             pltpu.VMEM(basis_series.shape, basis_series.dtype),
             pltpu.VMEM(bank.shape, bank.dtype),
             pltpu.VMEM((count, dets, rows * 2, basis), jnp.bfloat16),
@@ -274,7 +278,7 @@
             pltpu.VMEM((dets, total + SLIDE_BLOCKS * wins, rows, WIN), jnp.float32),
             pltpu.VMEM((total // per_row, 1, WIN), jnp.float32),
             pltpu.VMEM((count, 1, WIN), jnp.float32),
-            pltpu.SemaphoreType.DMA((2,)),
+            pltpu.SemaphoreType.DMA((3,)),
             pltpu.SemaphoreType.DMA((chips,)),
         ] + [pltpu.SemaphoreType.DMA((count,)) for _ in range(8)],
         compiler_params=pltpu.CompilerParams(

time: 36.6 us -> 35.9 us (0.981)
  Pallas kernels: 35.1 us -> 34.4 us
    pallas_call x1, Pallas kernels: 35.1 us -> 34.4 us  [per_device(): pl.pallas_call(functools.partial(kernel, chips, cores), out_shape=jax.Sha...]
where the time goes in v4:
time: 35.9 us; the launch traced here: 35.7 us
  Pallas kernels  34.4 us (96%)
  local copies, waits for them, and re-layouts  1.28 us (4%)
    pallas_call x1, Pallas kernels, per_device(): pl.pallas_call(functools.partial(kernel, chips, cores), out_shape=jax.Sha...  34.4 us
    unnamed x1, local copies, waits for them, and re-layouts  1.28 us

profile of v4, /device:TPU:0, one launch (start us, length us, event | category | flops | bytes accessed | tf_op | source)
XLA Modules:
  0.0 35.7 jit_solution(4185128136664814951)
XLA Ops:
  0.0 34.4 %shard_map.37 = f32[8,128]{1,0:T(8,128)} custom-call(s32[3]{0:T(128)} %off_hbm.1, bf16[3,128,1024]{2,1,0:T(8,128)(2,1)} %basis_hbm.1, bf16[3,32,128]{2,1,0:T(8,128)(2,1)} %bitcast.2), custom_call_target="tpu_custom_call" | custom-call | tf_op jit(solution)/shard_map/pallas_call | solution.py:265
  34.4 1.3 %copy.5 = f32[128,8]{0,1:T(8,128)} copy(f32[128,8]{0,1:T(8,128)} %bitcast.3) | data formatting | bytes 8192

commit v5 on v4

--- a/solution.py
+++ b/solution.py
@@ -209,7 +209,7 @@
 
     lane = lax.broadcasted_iota(jnp.int32, (per_row, rows, WIN), 2)
 
-    @pl.loop(0, total // per_row, unroll=4)
+    @pl.loop(0, total // per_row, unroll=8)
     def _(g):
         power = None
         for d in range(dets):

time: 35.9 us -> 35.8 us (level)
  no operation moved by 1% of the time
where the time goes in v5:
time: 35.8 us; the launch traced here: 35.6 us
  Pallas kernels  34.3 us (96%)
  local copies, waits for them, and re-layouts  1.28 us (4%)
    pallas_call x1, Pallas kernels, per_device(): pl.pallas_call(functools.partial(kernel, chips, cores), out_shape=jax.Sha...  34.3 us
    unnamed x1, local copies, waits for them, and re-layouts  1.28 us

profile of v5, /device:TPU:0, one launch (start us, length us, event | category | flops | bytes accessed | tf_op | source)
XLA Modules:
  0.0 35.6 jit_solution(13174982901412629708)
XLA Ops:
  0.0 34.3 %shard_map.37 = f32[8,128]{1,0:T(8,128)} custom-call(s32[3]{0:T(128)} %off_hbm.1, bf16[3,128,1024]{2,1,0:T(8,128)(2,1)} %basis_hbm.1, bf16[3,32,128]{2,1,0:T(8,128)(2,1)} %bitcast.2), custom_call_target="tpu_custom_call" | custom-call | tf_op jit(solution)/shard_map/pallas_call | solution.py:265
  34.3 1.3 %copy.5 = f32[128,8]{0,1:T(8,128)} copy(f32[128,8]{0,1:T(8,128)} %bitcast.3) | data formatting | bytes 8192
